TPU v7x, 32 devices: a whole 2x2x4 slice. The times are simulated.
32 devices in a mesh: groups: 2 (over x), seq: 4 (over y, core), head: 4 (over z).
Axes of the slice: x: 2, y: 2, z: 4, core: 2. Of those that a mesh axis runs over, the one named last changes fastest.
Arguments:
- query: bfloat16 [32, 16, 1024], P('groups', None, 'head'), parts along dimension 0, may hold values from -6 to 6, as said below
- new_key: bfloat16 [32, 16, 1024], P('groups', None, 'head'), parts along dimension 0, may hold values from -6 to 6
- new_value: bfloat16 [32, 16, 1024], P('groups', None, 'head'), parts along dimension 0, may hold values from -6 to 6
- keys: bfloat16 [32, 4096, 1024], P('groups', 'seq', 'head'), parts along dimension 0, may hold values from -6 to 6, as said below
- values: bfloat16 [32, 4096, 1024], P('groups', 'seq', 'head'), parts along dimension 0, may hold values from -6 to 6
- lengths: int32 [32], P('groups'), parts along dimension 0, may hold values from 2 to 4096
- time_bucket: int32 [32, 4096], P('groups', 'seq'), parts along dimension 0, may hold values from 0 to 63
- action: int32 [32, 4096], P('groups', 'seq'), parts along dimension 0, may hold values from 0 to 15
- time_bias: float32 [64, 8], P(None, 'head'), may hold values from -0.25 to 0.25
- action_bias: float32 [16, 8], P(None, 'head'), may hold values from -0.25 to 0.25
- gate: bfloat16 [32, 16, 1024], P('groups', None, 'head'), parts along dimension 0, may hold values from -6 to 6
- norm_gain: float32 [1024], P('head'), may hold values from 0.1 to 1.9
- w_out: bfloat16 [1024, 1024], P('head'), may hold values from -0.1875 to 0.1875
Outputs:
- output: bfloat16 [32, 16, 1024], P(('groups', 'seq'), None, 'head'), parts along dimension 0
There are 2 independent parts, one for each index of `groups`. A program takes and returns all parts, laid end to end along the dimension named above; an argument that names none is the same for every part. Nothing has to cross between parts.
Inputs may be any that keep to these rules, and one draw needn't show every extreme that they name: `query`: queries of order one; some users' queries may be large and equal to some of their keys. `keys`: keys of order one.
All inputs are finite; a program needn't handle non-finite values.
Results may differ from a plain program's by a relative error of at most 0.0056.
Values sent between devices are 32-bit elements; how exact they have to be, the bound alone decides.
A program may use at most 64 MiB of HBM per device.

v0:
```python
import functools
import math

import jax
import jax.numpy as jnp
from jax import lax
from jax.experimental import pallas as pl
from jax.experimental.pallas import tpu as pltpu
from jax.sharding import PartitionSpec as P

MESH = pl.DeviceIdType.MESH
LANES = 128
LOG2E = math.log2(math.e)
AHEAD = 4
INVALID = -1e30
FLOOR = -1e29
NT = (((1,), (1,)), ((), ()))


def partner(rank, step, count):
    result, bit = 0, 1
    while bit < count:
        held = (rank // bit) % 2
        result = result + bit * (1 - held if (step // bit) % 2 else held)
        bit *= 2
    return result


def column_to_row(column, first, lanes):
    shape = (column.shape[0], lanes)
    row_id = lax.broadcasted_iota(jnp.int32, shape, 0)
    lane_id = lax.broadcasted_iota(jnp.int32, shape, 1)
    return jnp.sum(jnp.where(lane_id == row_id + first, column, 0.0), axis=0, keepdims=True)


def row_to_column(row, first, count):
    shape = (count, row.shape[1])
    row_id = lax.broadcasted_iota(jnp.int32, shape, 0)
    lane_id = lax.broadcasted_iota(jnp.int32, shape, 1)
    return jnp.sum(jnp.where(lane_id == row_id + first, row, 0.0), axis=1, keepdims=True)


def kernel(
    dims,
    len_hbm,
    q_hbm,
    nk_hbm,
    nv_hbm,
    k_hbm,
    v_hbm,
    bucket_hbm,
    action_hbm,
    tb_hbm,
    ab_hbm,
    gate_hbm,
    gain_hbm,
    w_hbm,
    out_ref,
    len_ref,
    q_s,
    nk_s,
    nv_s,
    k_s,
    v_s,
    bucket_s,
    action_s,
    tb_s,
    ab_s,
    gate_s,
    gain_s,
    w_s,
    bias_s,
    part_s,
    got_s,
    zpart_s,
    zgot_s,
    square_s,
    squares_s,
    k_sem,
    v_sem,
    in_sem,
    late_sem,
    send_sem,
    recv_sem,
    zsend_sem,
    zrecv_sem,
    tsend_sem,
    trecv_sem,
):
    users, cands, block, heads, size, seqs, slices, local, out_cols = dims
    rows = heads * cands
    width = heads * size
    me = lax.axis_index("seq")
    mh = lax.axis_index("head")
    scale = LOG2E / math.sqrt(size)

    barrier = pltpu.get_barrier_semaphore()
    for step in range(1, seqs):
        pl.semaphore_signal(
            barrier, inc=1, device_id={"seq": partner(me, step, seqs)}, device_id_type=MESH
        )
    for step in range(1, slices):
        pl.semaphore_signal(
            barrier, inc=1, device_id={"head": (mh + step) % slices}, device_id_type=MESH
        )

    early = [
        pltpu.make_async_copy(source, target, in_sem.at[i])
        for i, (source, target) in enumerate(
            (
                (len_hbm, len_ref),
                (tb_hbm, tb_s),
                (ab_hbm, ab_s),
                (bucket_hbm, bucket_s),
                (action_hbm, action_s),
                (q_hbm, q_s),
            )
        )
    ]
    mine = pl.ds(me * local, local)
    late = [
        pltpu.make_async_copy(source, target, late_sem.at[i])
        for i, (source, target) in enumerate(
            (
                (nk_hbm.at[mine], nk_s),
                (nv_hbm.at[mine], nv_s),
                (gate_hbm.at[mine], gate_s),
                (gain_hbm, gain_s),
                (w_hbm, w_s),
            )
        )
    ]
    for copy in early:
        copy.start()
    order = []
    for turn in range(local):
        for step in range(seqs - 1, -1, -1):
            slot = len(order)
            user = partner(me, step, seqs) * local + turn
            k_copy = pltpu.make_async_copy(k_hbm.at[user], k_s.at[slot], k_sem.at[slot])
            v_copy = pltpu.make_async_copy(v_hbm.at[user], v_s.at[slot], v_sem.at[slot])
            order.append((turn, step, user, k_copy, v_copy))

    def fetch(slot):
        if slot < users:
            order[slot][3].start()
            order[slot][4].start()

    for slot in range(AHEAD):
        fetch(slot)

    square_s[...] = jnp.zeros_like(square_s)
    for copy in early:
        copy.wait()

    def table(ref, head):
        row = ref[head : head + 1, :] * LOG2E
        return jnp.concatenate([row, jnp.zeros((1, LANES - row.shape[1]), row.dtype)], axis=1)

    for head in range(heads):
        tb_row = jnp.broadcast_to(table(tb_s, head), (users, LANES))
        ab_row = jnp.broadcast_to(table(ab_s, head), (users, LANES))
        for chunk in range(block // LANES):
            lanes = slice(chunk * LANES, (chunk + 1) * LANES)
            bias_s[head, :, lanes] = jnp.take_along_axis(
                tb_row, bucket_s[:, lanes], axis=1
            ) + jnp.take_along_axis(ab_row, action_s[:, lanes], axis=1)

    position = me * block + lax.broadcasted_iota(jnp.int32, (1, block), 1)
    lane_of = lax.broadcasted_iota(jnp.int32, (cands, width), 1)

    def split_query(query):
        return jnp.concatenate(
            [
                jnp.where(lane_of // size == head, query, jnp.zeros_like(query))
                for head in range(heads)
            ],
            axis=0,
        )

    def attend(slot):
        turn, step, user, _, _ = order[slot]
        raw = lax.dot_general(
            split_query(q_s[user]), k_s[slot], NT, preferred_element_type=jnp.float32
        )
        valid = position < len_ref[user]
        bias = jnp.concatenate(
            [
                jnp.broadcast_to(
                    jnp.where(valid, bias_s[head, pl.ds(user, 1), :], INVALID), (cands, block)
                )
                for head in range(heads)
            ],
            axis=0,
        )
        scores = raw * scale + bias
        top = jnp.maximum(jnp.max(scores, axis=1, keepdims=True), FLOOR)
        weights = jnp.exp2(scores - top)
        total = jnp.sum(weights, axis=1, keepdims=True)
        mixed = jnp.dot(
            weights.astype(jnp.bfloat16), v_s[slot], preferred_element_type=jnp.float32
        )
        for head in range(heads):
            held = slice(head * cands, (head + 1) * cands)
            part_s[turn, step, held, :] = mixed[held, head * size : (head + 1) * size]
        stats = column_to_row(top, 0, size) + column_to_row(total, rows, size)
        part_s[turn, step, rows : rows + 8, :] = jnp.broadcast_to(stats, (8, size))

    def exchange(turn, step):
        return pltpu.make_async_remote_copy(
            src_ref=part_s.at[turn, step],
            dst_ref=got_s.at[turn, step - 1],
            send_sem=send_sem.at[turn, step - 1],
            recv_sem=recv_sem.at[turn, step - 1],
            device_id={"seq": partner(me, step, seqs)},
            device_id_type=MESH,
        )

    def spread(turn, step):
        target = (mh + step) % slices
        return pltpu.make_async_remote_copy(
            src_ref=zpart_s.at[turn, target],
            dst_ref=zgot_s.at[turn, step - 1],
            send_sem=zsend_sem.at[turn, step - 1],
            recv_sem=zrecv_sem.at[turn, step - 1],
            device_id={"head": target},
            device_id_type=MESH,
        )

    def tell(step):
        return pltpu.make_async_remote_copy(
            src_ref=square_s,
            dst_ref=squares_s.at[step - 1],
            send_sem=tsend_sem.at[step - 1],
            recv_sem=trecv_sem.at[step - 1],
            device_id={"head": (mh + step) % slices},
            device_id_type=MESH,
        )

    def combine(turn):
        for step in range(1, seqs):
            exchange(turn, step).wait_recv()
        blocks = [part_s.at[turn, 0]] + [got_s.at[turn, step - 1] for step in range(1, seqs)]
        query = q_s[me * local + turn].astype(jnp.float32)
        new_key = nk_s[turn].astype(jnp.float32)
        new_value = nv_s[turn].astype(jnp.float32)
        product = query * new_key

        def by_head(source):
            return jnp.concatenate(
                [source[:, head * size : (head + 1) * size] for head in range(heads)], axis=0
            )

        own = jnp.sum(by_head(product), axis=1, keepdims=True) * scale
        maxima = [row_to_column(ref[rows : rows + 1, :], 0, rows) for ref in blocks]
        sums = [row_to_column(ref[rows : rows + 1, :], rows, rows) for ref in blocks]
        top = functools.reduce(jnp.maximum, maxima, own)
        own_factor = jnp.exp2(own - top)
        numer = own_factor * by_head(new_value)
        denom = own_factor
        for ref, high, amount in zip(blocks, maxima, sums):
            factor = jnp.exp2(high - top)
            numer = numer + factor * ref[:rows, :]
            denom = denom + factor * amount
        attended = numer / denom
        squares = jnp.sum(jnp.square(attended), axis=1, keepdims=True)
        square = squares[:cands]
        for head in range(1, heads):
            square = square + squares[head * cands : (head + 1) * cands]
        square_s[turn : turn + 1, :] = column_to_row(square, 0, LANES)
        if turn == local - 1:
            for step in range(1, slices):
                tell(step).start()
        wide = jnp.concatenate(
            [attended[head * cands : (head + 1) * cands] for head in range(heads)], axis=1
        )
        gate = gate_s[turn].astype(jnp.float32)
        gain = gain_s[...].reshape(1, width)
        hidden = (wide * gain * (gate / (1.0 + jnp.exp(-gate)))).astype(jnp.bfloat16)
        projected = jnp.dot(hidden, w_s[...], preferred_element_type=jnp.float32)
        for target in range(slices):
            zpart_s[turn, target] = projected[:, target * out_cols : (target + 1) * out_cols]
        for step in range(slices - 1, 0, -1):
            spread(turn, step).start()

    def finish(turn):
        total = zpart_s[turn, mh]
        for step in range(1, slices):
            spread(turn, step).wait_recv()
            total = total + zgot_s[turn, step - 1]
        out_ref[turn] = (total * factor_of(turn)).astype(out_ref.dtype)

    for turn in range(local):
        for step in range(seqs - 1, -1, -2):
            slots = [turn * seqs + seqs - 1 - step]
            if step:
                slots.append(slots[0] + 1)
            for slot in slots:
                order[slot][3].wait()
                order[slot][4].wait()
            for slot in slots:
                fetch(slot + AHEAD)
            if turn == 0 and step == seqs - 1:
                for copy in late:
                    copy.start()
            for slot in slots:
                attend(slot)
            if turn == 0 and step == seqs - 1:
                pl.semaphore_wait(barrier, seqs - 1 + slices - 1)
            for slot in slots:
                if order[slot][1]:
                    exchange(turn, order[slot][1]).start()
            if turn > 0 and step == seqs - 1:
                if turn == 1:
                    for copy in late:
                        copy.wait()
                combine(turn - 1)
    if local == 1:
        for copy in late:
            copy.wait()
    combine(local - 1)
    for step in range(1, slices):
        tell(step).wait_recv()
    square = square_s[...]
    for step in range(1, slices):
        square = square + squares_s[step - 1]

    def factor_of(turn):
        column = row_to_column(square[turn : turn + 1, :], 0, cands)
        return 1.0 / jnp.sqrt(column / (width * slices) + 1e-6)

    for turn in range(local):
        finish(turn)
    for step in range(1, slices):
        tell(step).wait_send()
    for turn in range(local):
        for step in range(1, seqs):
            exchange(turn, step).wait_send()
        for step in range(1, slices):
            spread(turn, step).wait_send()


def body(
    query,
    new_key,
    new_value,
    keys,
    values,
    lengths,
    time_bucket,
    action,
    time_bias,
    action_bias,
    gate,
    norm_gain,
    w_out,
):
    users, block, width = keys.shape
    cands = query.shape[1]
    heads = time_bias.shape[1]
    size = width // heads
    seqs = lax.axis_size("seq")
    slices = lax.axis_size("head")
    local = users // seqs
    rows = heads * cands
    lines = -(-local // 8) * 8
    out_cols = w_out.shape[1] // slices
    dims = (users, cands, block, heads, size, seqs, slices, local, out_cols)
    f32, bf16 = jnp.float32, jnp.bfloat16
    anywhere = pl.BlockSpec(memory_space=pltpu.HBM)
    return pl.pallas_call(
        functools.partial(kernel, dims),
        out_shape=jax.ShapeDtypeStruct((local, cands, out_cols), bf16),
        in_specs=[anywhere] * 13,
        out_specs=pl.BlockSpec(memory_space=pltpu.VMEM),
        scratch_shapes=[
            pltpu.SMEM((users,), jnp.int32),
            pltpu.VMEM((users, cands, width), bf16),
            pltpu.VMEM((local, cands, width), bf16),
            pltpu.VMEM((local, cands, width), bf16),
            pltpu.VMEM((users, block, width), bf16),
            pltpu.VMEM((users, block, width), bf16),
            pltpu.VMEM((users, block), jnp.int32),
            pltpu.VMEM((users, block), jnp.int32),
            pltpu.VMEM(time_bias.T.shape, f32),
            pltpu.VMEM(action_bias.T.shape, f32),
            pltpu.VMEM((local, cands, width), bf16),
            pltpu.VMEM((width,), f32),
            pltpu.VMEM(w_out.shape, bf16),
            pltpu.VMEM((heads, users, block), f32),
            pltpu.VMEM((local, seqs, rows + 8, size), f32),
            pltpu.VMEM((local, seqs - 1, rows + 8, size), f32),
            pltpu.VMEM((local, slices, cands, out_cols), f32),
            pltpu.VMEM((local, slices - 1, cands, out_cols), f32),
            pltpu.VMEM((lines, LANES), f32),
            pltpu.VMEM((slices - 1, lines, LANES), f32),
            pltpu.SemaphoreType.DMA((users,)),
            pltpu.SemaphoreType.DMA((users,)),
            pltpu.SemaphoreType.DMA((6,)),
            pltpu.SemaphoreType.DMA((5,)),
            pltpu.SemaphoreType.DMA((local, seqs - 1)),
            pltpu.SemaphoreType.DMA((local, seqs - 1)),
            pltpu.SemaphoreType.DMA((local, slices - 1)),
            pltpu.SemaphoreType.DMA((local, slices - 1)),
            pltpu.SemaphoreType.DMA((slices - 1,)),
            pltpu.SemaphoreType.DMA((slices - 1,)),
        ],
        compiler_params=pltpu.CompilerParams(
            collective_id=0, has_side_effects=True, vmem_limit_bytes=67043328
        ),
    )(
        lengths,
        query,
        new_key,
        new_value,
        keys,
        values,
        time_bucket,
        action,
        time_bias.T,
        action_bias.T,
        gate,
        norm_gain,
        w_out,
    )


def solution(mesh):
    placed = (
        P("groups", None, "head"),
        P("groups", None, "head"),
        P("groups", None, "head"),
        P("groups", "seq", "head"),
        P("groups", "seq", "head"),
        P("groups"),
        P("groups", "seq"),
        P("groups", "seq"),
        P(None, "head"),
        P(None, "head"),
        P("groups", None, "head"),
        P("head"),
        P("head", None),
    )
    return jax.shard_map(
        body,
        mesh=mesh,
        in_specs=placed,
        out_specs=P(("groups", "seq"), None, "head"),
        check_vma=False,
    )
```

profile of v0, /device:TPU:0, one launch (start us, length us, event | category | flops | bytes accessed | tf_op | source)
XLA Modules:
  0.0 24.5 jit_solution(10378261460086923789)
XLA Ops:
  0.0 23.1 %shard_map.127 = bf16[4,16,256]{2,1,0:T(8,128)(2,1)} custom-call(s32[16]{0:T(128)} %len_hbm.1, bf16[16,16,256]{2,1,0:T(8,128)(2,1)} %q_hbm.1, bf16[16,16,256]{2,1,0:T(8,128)(2,1)} %nk_hbm.1, bf16[16,16,256]{2,1,0:T(8,128)(2,1)} %nv_hbm.1, bf16[16,1024,256]{2,1,0:T(8,128)(2,1)} %k_hbm.1, bf16[16,1024,256]{2,1,0:T(8,128)(2,1)} %v_hbm.1, ...), custom_call_target="tpu_custom_call" | custom-call | tf_op jit(solution)/shard_map/pallas_call | solution.py:371
  23.1 1.4 %copy.15 = bf16[4,16,256]{2,1,0:T(8,128)(2,1)} copy(bf16[4,16,256]{2,1,0:T(8,128)(2,1)} %shard_map.127) | data formatting | bytes 65536
where the time goes:
time: 24.7 us; the launch traced here: 24.5 us
  Pallas kernels  23.1 us (94%)
  local copies, waits for them, and re-layouts  1.38 us (6%)
    pallas_call x1, Pallas kernels, body(): pl.pallas_call(functools.partial(kernel, dims), out_shape=jax.ShapeDtypeS...  23.1 us
    unnamed x1, local copies, waits for them, and re-layouts  1.38 us

commit v1 on v0

--- a/solution.py
+++ b/solution.py
@@ -11,7 +11,8 @@
 MESH = pl.DeviceIdType.MESH
 LANES = 128
 LOG2E = math.log2(math.e)
-AHEAD = 4
+GROUP = 2
+LAG = 2
 INVALID = -1e30
 FLOOR = -1e29
 NT = (((1,), (1,)), ((), ()))
@@ -69,13 +70,12 @@
     gate_s,
     gain_s,
     w_s,
+    qd_s,
     bias_s,
     part_s,
     got_s,
     zpart_s,
     zgot_s,
-    square_s,
-    squares_s,
     k_sem,
     v_sem,
     in_sem,
@@ -84,8 +84,6 @@
     recv_sem,
     zsend_sem,
     zrecv_sem,
-    tsend_sem,
-    trecv_sem,
 ):
     users, cands, block, heads, size, seqs, slices, local, out_cols = dims
     rows = heads * cands
@@ -140,55 +138,46 @@
             k_copy = pltpu.make_async_copy(k_hbm.at[user], k_s.at[slot], k_sem.at[slot])
             v_copy = pltpu.make_async_copy(v_hbm.at[user], v_s.at[slot], v_sem.at[slot])
             order.append((turn, step, user, k_copy, v_copy))
-
-    def fetch(slot):
-        if slot < users:
-            order[slot][3].start()
-            order[slot][4].start()
-
-    for slot in range(AHEAD):
-        fetch(slot)
-
-    square_s[...] = jnp.zeros_like(square_s)
+    for _, _, _, k_copy, v_copy in order:
+        k_copy.start(priority=1)
+        v_copy.start(priority=1)
+    for copy in late:
+        copy.start()
     for copy in early:
         copy.wait()
+
+    lane_of = lax.broadcasted_iota(jnp.int32, (users, cands, width), 2)
+    query = q_s[...]
+    for head in range(heads):
+        qd_s[:, head * cands : (head + 1) * cands, :] = jnp.where(
+            lane_of // size == head, query, jnp.zeros_like(query)
+        )
 
     def table(ref, head):
         row = ref[head : head + 1, :] * LOG2E
         return jnp.concatenate([row, jnp.zeros((1, LANES - row.shape[1]), row.dtype)], axis=1)
 
+    user_id = lax.broadcasted_iota(jnp.int32, (users, LANES), 0)
+    limit = jnp.zeros((users, LANES), jnp.int32)
+    for user in range(users):
+        limit = jnp.where(user_id == user, len_ref[user], limit)
+    limit = limit - me * block - lax.broadcasted_iota(jnp.int32, (users, LANES), 1)
     for head in range(heads):
         tb_row = jnp.broadcast_to(table(tb_s, head), (users, LANES))
         ab_row = jnp.broadcast_to(table(ab_s, head), (users, LANES))
         for chunk in range(block // LANES):
             lanes = slice(chunk * LANES, (chunk + 1) * LANES)
-            bias_s[head, :, lanes] = jnp.take_along_axis(
-                tb_row, bucket_s[:, lanes], axis=1
-            ) + jnp.take_along_axis(ab_row, action_s[:, lanes], axis=1)
-
-    position = me * block + lax.broadcasted_iota(jnp.int32, (1, block), 1)
-    lane_of = lax.broadcasted_iota(jnp.int32, (cands, width), 1)
-
-    def split_query(query):
-        return jnp.concatenate(
-            [
-                jnp.where(lane_of // size == head, query, jnp.zeros_like(query))
-                for head in range(heads)
-            ],
-            axis=0,
-        )
-
-    def attend(slot):
+            bias = jnp.take_along_axis(tb_row, bucket_s[:, lanes], axis=1) + jnp.take_along_axis(
+                ab_row, action_s[:, lanes], axis=1
+            )
+            bias_s[head, :, lanes] = jnp.where(limit > chunk * LANES, bias, INVALID)
+
+    def score(slot):
         turn, step, user, _, _ = order[slot]
-        raw = lax.dot_general(
-            split_query(q_s[user]), k_s[slot], NT, preferred_element_type=jnp.float32
-        )
-        valid = position < len_ref[user]
+        raw = lax.dot_general(qd_s[user], k_s[slot], NT, preferred_element_type=jnp.float32)
         bias = jnp.concatenate(
             [
-                jnp.broadcast_to(
-                    jnp.where(valid, bias_s[head, pl.ds(user, 1), :], INVALID), (cands, block)
-                )
+                jnp.broadcast_to(bias_s[head, pl.ds(user, 1), :], (cands, block))
                 for head in range(heads)
             ],
             axis=0,
@@ -197,14 +186,25 @@
         top = jnp.maximum(jnp.max(scores, axis=1, keepdims=True), FLOOR)
         weights = jnp.exp2(scores - top)
         total = jnp.sum(weights, axis=1, keepdims=True)
-        mixed = jnp.dot(
-            weights.astype(jnp.bfloat16), v_s[slot], preferred_element_type=jnp.float32
-        )
+        stats = column_to_row(top, 0, size) + column_to_row(total, rows, size)
+        part_s[turn, step, rows : rows + 1, :] = stats
+        return weights.astype(jnp.bfloat16)
+
+    def mix(slot, weights):
+        turn, step, _, _, _ = order[slot]
+        mixed = jnp.dot(weights, v_s[slot], preferred_element_type=jnp.float32)
         for head in range(heads):
             held = slice(head * cands, (head + 1) * cands)
             part_s[turn, step, held, :] = mixed[held, head * size : (head + 1) * size]
-        stats = column_to_row(top, 0, size) + column_to_row(total, rows, size)
-        part_s[turn, step, rows : rows + 8, :] = jnp.broadcast_to(stats, (8, size))
+
+    def attend(slots):
+        waiting = []
+        for slot in slots:
+            waiting.append((slot, score(slot)))
+            if len(waiting) > 1:
+                mix(*waiting.pop(0))
+        for item in waiting:
+            mix(*item)
 
     def exchange(turn, step):
         return pltpu.make_async_remote_copy(
@@ -227,31 +227,22 @@
             device_id_type=MESH,
         )
 
-    def tell(step):
-        return pltpu.make_async_remote_copy(
-            src_ref=square_s,
-            dst_ref=squares_s.at[step - 1],
-            send_sem=tsend_sem.at[step - 1],
-            recv_sem=trecv_sem.at[step - 1],
-            device_id={"head": (mh + step) % slices},
-            device_id_type=MESH,
+    def by_head(source):
+        return jnp.concatenate(
+            [source[:, head * size : (head + 1) * size] for head in range(heads)], axis=0
         )
 
     def combine(turn):
+        query = q_s[me * local + turn].astype(jnp.float32)
+        new_key = nk_s[turn].astype(jnp.float32)
+        new_value = nv_s[turn].astype(jnp.float32)
+        own = jnp.sum(by_head(query * new_key), axis=1, keepdims=True) * scale
+        gate = gate_s[turn].astype(jnp.float32)
+        gain = gain_s[...].reshape(1, width)
+        gated = gain * (gate / (1.0 + jnp.exp(-gate)))
         for step in range(1, seqs):
             exchange(turn, step).wait_recv()
         blocks = [part_s.at[turn, 0]] + [got_s.at[turn, step - 1] for step in range(1, seqs)]
-        query = q_s[me * local + turn].astype(jnp.float32)
-        new_key = nk_s[turn].astype(jnp.float32)
-        new_value = nv_s[turn].astype(jnp.float32)
-        product = query * new_key
-
-        def by_head(source):
-            return jnp.concatenate(
-                [source[:, head * size : (head + 1) * size] for head in range(heads)], axis=0
-            )
-
-        own = jnp.sum(by_head(product), axis=1, keepdims=True) * scale
         maxima = [row_to_column(ref[rows : rows + 1, :], 0, rows) for ref in blocks]
         sums = [row_to_column(ref[rows : rows + 1, :], rows, rows) for ref in blocks]
         top = functools.reduce(jnp.maximum, maxima, own)
@@ -267,19 +258,17 @@
         square = squares[:cands]
         for head in range(1, heads):
             square = square + squares[head * cands : (head + 1) * cands]
-        square_s[turn : turn + 1, :] = column_to_row(square, 0, LANES)
-        if turn == local - 1:
-            for step in range(1, slices):
-                tell(step).start()
         wide = jnp.concatenate(
             [attended[head * cands : (head + 1) * cands] for head in range(heads)], axis=1
         )
-        gate = gate_s[turn].astype(jnp.float32)
-        gain = gain_s[...].reshape(1, width)
-        hidden = (wide * gain * (gate / (1.0 + jnp.exp(-gate)))).astype(jnp.bfloat16)
+        hidden = (wide * gated).astype(jnp.bfloat16)
         projected = jnp.dot(hidden, w_s[...], preferred_element_type=jnp.float32)
+        square_row = column_to_row(square, 0, out_cols)
         for target in range(slices):
-            zpart_s[turn, target] = projected[:, target * out_cols : (target + 1) * out_cols]
+            zpart_s[turn, target, :cands, :] = projected[
+                :, target * out_cols : (target + 1) * out_cols
+            ]
+            zpart_s[turn, target, cands : cands + 1, :] = square_row
         for step in range(slices - 1, 0, -1):
             spread(turn, step).start()
 
@@ -288,51 +277,35 @@
         for step in range(1, slices):
             spread(turn, step).wait_recv()
             total = total + zgot_s[turn, step - 1]
-        out_ref[turn] = (total * factor_of(turn)).astype(out_ref.dtype)
-
-    for turn in range(local):
-        for step in range(seqs - 1, -1, -2):
-            slots = [turn * seqs + seqs - 1 - step]
-            if step:
-                slots.append(slots[0] + 1)
-            for slot in slots:
-                order[slot][3].wait()
-                order[slot][4].wait()
-            for slot in slots:
-                fetch(slot + AHEAD)
-            if turn == 0 and step == seqs - 1:
-                for copy in late:
-                    copy.start()
-            for slot in slots:
-                attend(slot)
-            if turn == 0 and step == seqs - 1:
-                pl.semaphore_wait(barrier, seqs - 1 + slices - 1)
-            for slot in slots:
-                if order[slot][1]:
-                    exchange(turn, order[slot][1]).start()
-            if turn > 0 and step == seqs - 1:
-                if turn == 1:
-                    for copy in late:
-                        copy.wait()
-                combine(turn - 1)
-    if local == 1:
-        for copy in late:
-            copy.wait()
-    combine(local - 1)
-    for step in range(1, slices):
-        tell(step).wait_recv()
-    square = square_s[...]
-    for step in range(1, slices):
-        square = square + squares_s[step - 1]
-
-    def factor_of(turn):
-        column = row_to_column(square[turn : turn + 1, :], 0, cands)
-        return 1.0 / jnp.sqrt(column / (width * slices) + 1e-6)
-
+        column = row_to_column(total[cands : cands + 1, :], 0, cands)
+        factor = 1.0 / jnp.sqrt(column / (width * slices) + 1e-6)
+        out_ref[turn] = (total[:cands] * factor).astype(out_ref.dtype)
+
+    groups = [
+        list(range(first, min(first + GROUP, len(order)))) for first in range(0, len(order), GROUP)
+    ]
+    done = 0
+    for index, slots in enumerate(groups):
+        for slot in slots:
+            order[slot][3].wait()
+            order[slot][4].wait()
+        attend(slots)
+        if index == 0:
+            pl.semaphore_wait(barrier, seqs - 1 + slices - 1)
+        for slot in slots:
+            if order[slot][1]:
+                exchange(order[slot][0], order[slot][1]).start()
+        if index == 0:
+            for copy in late:
+                copy.wait()
+        while done < local and (done + 1) * seqs + LAG * GROUP <= slots[-1] + 1:
+            combine(done)
+            done += 1
+    while done < local:
+        combine(done)
+        done += 1
     for turn in range(local):
         finish(turn)
-    for step in range(1, slices):
-        tell(step).wait_send()
     for turn in range(local):
         for step in range(1, seqs):
             exchange(turn, step).wait_send()
@@ -363,7 +336,6 @@
     slices = lax.axis_size("head")
     local = users // seqs
     rows = heads * cands
-    lines = -(-local // 8) * 8
     out_cols = w_out.shape[1] // slices
     dims = (users, cands, block, heads, size, seqs, slices, local, out_cols)
     f32, bf16 = jnp.float32, jnp.bfloat16
@@ -387,13 +359,12 @@
             pltpu.VMEM((local, cands, width), bf16),
             pltpu.VMEM((width,), f32),
             pltpu.VMEM(w_out.shape, bf16),
+            pltpu.VMEM((users, rows, width), bf16),
             pltpu.VMEM((heads, users, block), f32),
-            pltpu.VMEM((local, seqs, rows + 8, size), f32),
-            pltpu.VMEM((local, seqs - 1, rows + 8, size), f32),
-            pltpu.VMEM((local, slices, cands, out_cols), f32),
-            pltpu.VMEM((local, slices - 1, cands, out_cols), f32),
-            pltpu.VMEM((lines, LANES), f32),
-            pltpu.VMEM((slices - 1, lines, LANES), f32),
+            pltpu.VMEM((local, seqs, rows + 1, size), f32),
+            pltpu.VMEM((local, seqs - 1, rows + 1, size), f32),
+            pltpu.VMEM((local, slices, cands + 1, out_cols), f32),
+            pltpu.VMEM((local, slices - 1, cands + 1, out_cols), f32),
             pltpu.SemaphoreType.DMA((users,)),
             pltpu.SemaphoreType.DMA((users,)),
             pltpu.SemaphoreType.DMA((6,)),
@@ -402,26 +373,29 @@
             pltpu.SemaphoreType.DMA((local, seqs - 1)),
             pltpu.SemaphoreType.DMA((local, slices - 1)),
             pltpu.SemaphoreType.DMA((local, slices - 1)),
-            pltpu.SemaphoreType.DMA((slices - 1,)),
-            pltpu.SemaphoreType.DMA((slices - 1,)),
         ],
         compiler_params=pltpu.CompilerParams(
-            collective_id=0, has_side_effects=True, vmem_limit_bytes=67043328
+            collective_id=0, has_side_effects=True, vmem_limit_bytes=52428800
         ),
     )(
-        lengths,
-        query,
-        new_key,
-        new_value,
-        keys,
-        values,
-        time_bucket,
-        action,
-        time_bias.T,
-        action_bias.T,
-        gate,
-        norm_gain,
-        w_out,
+        *(
+            pltpu.with_memory_space_constraint(x, pltpu.HBM)
+            for x in (
+                lengths,
+                query,
+                new_key,
+                new_value,
+                keys,
+                values,
+                time_bucket,
+                action,
+                time_bias.T,
+                action_bias.T,
+                gate,
+                norm_gain,
+                w_out,
+            )
+        )
     )
 
 

time: 24.7 us -> 21.5 us (0.87)
  Pallas kernels: 23.1 us -> 20.7 us
  local copies, waits for them, and re-layouts: 1.38 us -> 0.62 us
    pallas_call x1, Pallas kernels: 23.1 us -> 20.7 us  [body(): pl.pallas_call(functools.partial(kernel, dims), out_shape=jax.ShapeDtypeS...]
    unnamed x1, local copies, waits for them, and re-layouts: 1.38 us -> 0.62 us
where the time goes in v1:
time: 21.5 us; the launch traced here: 21.4 us
  Pallas kernels  20.7 us (96%)
  local copies, waits for them, and re-layouts  0.62 us (3%)
    pallas_call x1, Pallas kernels, body(): pl.pallas_call(functools.partial(kernel, dims), out_shape=jax.ShapeDtypeS...  20.7 us
    unnamed x1, local copies, waits for them, and re-layouts  0.62 us

profile of v1, /device:TPU:0, one launch (start us, length us, event | category | flops | bytes accessed | tf_op | source)
XLA Modules:
  0.0 21.4 jit_solution(6343514970081700241)
XLA Ops:
  0.0 20.7 %shard_map.127 = bf16[4,16,256]{2,1,0:T(8,128)(2,1)S(1)} custom-call(s32[16]{0:T(128)} %len_hbm.1, bf16[16,16,256]{2,1,0:T(8,128)(2,1)} %q_hbm.1, bf16[16,16,256]{2,1,0:T(8,128)(2,1)} %nk_hbm.1, bf16[16,16,256]{2,1,0:T(8,128)(2,1)} %nv_hbm.1, bf16[16,1024,256]{2,1,0:T(8,128)(2,1)} %k_hbm.1, bf16[16,1024,256]{2,1,0:T(8,128)(2,1)} %v_hbm.1, ...), custom_call_target="tpu_custom_call" | custom-call | tf_op jit(solution)/shard_map/pallas_call | solution.py:343
  20.8 0.6 %copy.15 = bf16[4,16,256]{2,1,0:T(8,128)(2,1)} copy(bf16[4,16,256]{2,1,0:T(8,128)(2,1)S(1)} %shard_map.127) | data formatting | bytes 65536

commit v2 on v1

v2 whole, which is shorter than its diff:
```python
import functools
import math

import jax
import jax.numpy as jnp
from jax import lax
from jax.experimental import pallas as pl
from jax.experimental.pallas import tpu as pltpu
from jax.sharding import PartitionSpec as P

MESH = pl.DeviceIdType.MESH
LANES = 128
LOG2E = math.log2(math.e)
GROUP = 4
START = 13
INVALID = -1e30
FLOOR = -1e29
NT = (((1,), (1,)), ((), ()))


def partner(rank, step, count):
    result, bit = 0, 1
    while bit < count:
        held = (rank // bit) % 2
        result = result + bit * (1 - held if (step // bit) % 2 else held)
        bit *= 2
    return result


def plan(seqs, local):
    away = list(range(seqs - 1, 0, -1))
    groups = []
    for turn in range(local):
        steps = away + [0] if turn == 0 else away
        for first in range(0, len(steps), GROUP):
            groups.append([(turn, step) for step in steps[first : first + GROUP]])
    groups.extend([(turn, 0)] for turn in range(1, local))
    return groups


def column_to_row(column, first, lanes):
    shape = (column.shape[0], lanes)
    row_id = lax.broadcasted_iota(jnp.int32, shape, 0)
    lane_id = lax.broadcasted_iota(jnp.int32, shape, 1)
    return jnp.sum(jnp.where(lane_id == row_id + first, column, 0.0), axis=0, keepdims=True)


def row_to_column(row, first, count):
    shape = (count, row.shape[1])
    row_id = lax.broadcasted_iota(jnp.int32, shape, 0)
    lane_id = lax.broadcasted_iota(jnp.int32, shape, 1)
    return jnp.sum(jnp.where(lane_id == row_id + first, row, 0.0), axis=1, keepdims=True)


def kernel(
    dims,
    len_hbm,
    q_hbm,
    nk_hbm,
    nv_hbm,
    k_hbm,
    v_hbm,
    bucket_hbm,
    action_hbm,
    tb_hbm,
    ab_hbm,
    gate_hbm,
    gain_hbm,
    w_hbm,
    out_ref,
    len_ref,
    q_s,
    mine_s,
    kv_s,
    event_s,
    tb_s,
    ab_s,
    gain_s,
    w_s,
    qd_s,
    gated_s,
    bias_s,
    part_s,
    got_s,
    zpart_s,
    zgot_s,
    kv_sem,
    in_sem,
    late_sem,
    send_sem,
    recv_sem,
    zsend_sem,
    zrecv_sem,
):
    users, cands, block, heads, size, seqs, slices, local, out_cols = dims
    rows = heads * cands
    width = heads * size
    tiles = out_cols // LANES
    me = lax.axis_index("seq")
    mh = lax.axis_index("head")

    def landed(ref, sem):
        pltpu.make_async_copy(ref, ref, sem).wait()

    scale = LOG2E / math.sqrt(size)

    barrier = pltpu.get_barrier_semaphore()
    for step in range(1, seqs):
        pl.semaphore_signal(
            barrier, inc=1, device_id={"seq": partner(me, step, seqs)}, device_id_type=MESH
        )
    for step in range(1, slices):
        pl.semaphore_signal(
            barrier, inc=1, device_id={"head": partner(mh, step, slices)}, device_id_type=MESH
        )

    early = [
        pltpu.make_async_copy(source, target, in_sem.at[min(i, 4)])
        for i, (source, target) in enumerate(
            (
                (len_hbm, len_ref),
                (tb_hbm, tb_s),
                (ab_hbm, ab_s),
                (q_hbm, q_s),
                (bucket_hbm, event_s.at[0]),
                (action_hbm, event_s.at[1]),
            )
        )
    ]
    mine = pl.ds(me * local, local)
    late = [
        pltpu.make_async_copy(source, target, late_sem.at[min(i, 2)])
        for i, (source, target) in enumerate(
            (
                (gain_hbm, gain_s),
                (w_hbm, w_s),
                (nk_hbm.at[mine], mine_s.at[0]),
                (nv_hbm.at[mine], mine_s.at[1]),
                (gate_hbm.at[mine], mine_s.at[2]),
            )
        )
    ]
    for copy in early:
        copy.start()
    order = []
    groups = plan(seqs, local)
    for index, group in enumerate(groups):
        for turn, step in group:
            user = partner(me, step, seqs) * local + turn
            for part, source in enumerate((k_hbm, v_hbm)):
                pltpu.make_async_copy(
                    source.at[user], kv_s.at[len(order), part], kv_sem.at[index]
                ).start(priority=1)
            order.append((turn, step, user))
    for copy in late:
        copy.start()
    for copy in early[:4]:
        copy.wait()
    landed(event_s, in_sem.at[4])

    lane_of = lax.broadcasted_iota(jnp.int32, (users, cands, width), 2)
    query = q_s[...]
    for head in range(heads):
        qd_s[:, head * cands : (head + 1) * cands, :] = jnp.where(
            lane_of // size == head, query, jnp.zeros_like(query)
        )

    def table(ref, head):
        row = ref[head : head + 1, :] * LOG2E
        return jnp.concatenate([row, jnp.zeros((1, LANES - row.shape[1]), row.dtype)], axis=1)

    user_id = lax.broadcasted_iota(jnp.int32, (users, LANES), 0)
    limit = jnp.zeros((users, LANES), jnp.int32)
    for user in range(users):
        limit = jnp.where(user_id == user, len_ref[user], limit)
    limit = limit - me * block - lax.broadcasted_iota(jnp.int32, (users, LANES), 1)
    for head in range(heads):
        tb_row = jnp.broadcast_to(table(tb_s, head), (users, LANES))
        ab_row = jnp.broadcast_to(table(ab_s, head), (users, LANES))
        for chunk in range(block // LANES):
            lanes = slice(chunk * LANES, (chunk + 1) * LANES)
            bias = jnp.take_along_axis(tb_row, event_s[0, :, lanes], axis=1) + jnp.take_along_axis(
                ab_row, event_s[1, :, lanes], axis=1
            )
            bias_s[head, :, lanes] = jnp.where(limit > chunk * LANES, bias, INVALID)

    for copy in late[:2]:
        copy.wait()
    landed(mine_s, late_sem.at[2])
    gate = mine_s[2].astype(jnp.float32)
    gated_s[...] = gain_s[...].reshape(1, 1, width) * (gate / (1.0 + jnp.exp(-gate)))

    def by_head(source):
        return jnp.concatenate(
            [source[:, head * size : (head + 1) * size] for head in range(heads)], axis=0
        )

    def score(slot):
        turn, step, user = order[slot]
        raw = lax.dot_general(qd_s[user], kv_s[slot, 0], NT, preferred_element_type=jnp.float32)
        bias = jnp.concatenate(
            [
                jnp.broadcast_to(bias_s[head, pl.ds(user, 1), :], (cands, block))
                for head in range(heads)
            ],
            axis=0,
        )
        scores = raw * scale + bias
        top = jnp.maximum(jnp.max(scores, axis=1, keepdims=True), FLOOR)
        fresh = None
        if step == 0:
            product = q_s[user].astype(jnp.float32) * mine_s[0, turn].astype(jnp.float32)
            own = jnp.sum(by_head(product), axis=1, keepdims=True) * scale
            top = jnp.maximum(top, own)
            fresh = jnp.exp2(own - top)
        weights = jnp.exp2(scores - top)
        total = jnp.sum(weights, axis=1, keepdims=True)
        if step == 0:
            total = total + fresh
            fresh = fresh * by_head(mine_s[1, turn].astype(jnp.float32))
        stats = column_to_row(top, 0, size) + column_to_row(total, rows, size)
        part_s[turn, step, rows : rows + 1, :] = stats
        return weights.astype(jnp.bfloat16), fresh

    def mix(slot, weights, fresh):
        turn, step, _ = order[slot]
        mixed = jnp.dot(weights, kv_s[slot, 1], preferred_element_type=jnp.float32)
        for head in range(heads):
            held = slice(head * cands, (head + 1) * cands)
            piece = mixed[held, head * size : (head + 1) * size]
            part_s[turn, step, held, :] = piece if fresh is None else piece + fresh[held]

    def attend(slots):
        waiting = []
        for slot in slots:
            waiting.append((slot, *score(slot)))
            if len(waiting) > 1:
                mix(*waiting.pop(0))
        for item in waiting:
            mix(*item)

    def exchange(turn, step):
        return pltpu.make_async_remote_copy(
            src_ref=part_s.at[turn, step],
            dst_ref=got_s.at[turn, step - 1],
            send_sem=send_sem,
            recv_sem=recv_sem.at[turn],
            device_id={"seq": partner(me, step, seqs)},
            device_id_type=MESH,
        )

    def spread(turn, step):
        target = partner(mh, step, slices)
        return pltpu.make_async_remote_copy(
            src_ref=zpart_s.at[turn, target],
            dst_ref=zgot_s.at[turn, step - 1],
            send_sem=zsend_sem,
            recv_sem=zrecv_sem.at[turn],
            device_id={"head": target},
            device_id_type=MESH,
        )

    def combine(turn):
        landed(got_s.at[turn], recv_sem.at[turn])
        blocks = [part_s.at[turn, 0]] + [got_s.at[turn, step - 1] for step in range(1, seqs)]
        maxima = [row_to_column(ref[rows : rows + 1, :], 0, rows) for ref in blocks]
        sums = [row_to_column(ref[rows : rows + 1, :], rows, rows) for ref in blocks]
        top = functools.reduce(jnp.maximum, maxima)
        numer, denom = 0.0, 0.0
        for ref, high, amount in zip(blocks, maxima, sums):
            factor = jnp.exp2(high - top)
            numer = numer + factor * ref[:rows, :]
            denom = denom + factor * amount
        attended = numer / denom
        squares = jnp.sum(jnp.square(attended), axis=1, keepdims=True)
        square = squares[:cands]
        for head in range(1, heads):
            square = square + squares[head * cands : (head + 1) * cands]
        wide = jnp.concatenate(
            [attended[head * cands : (head + 1) * cands] for head in range(heads)], axis=1
        )
        hidden = (wide * gated_s[turn]).astype(jnp.bfloat16)
        projected = jnp.dot(hidden, w_s[...], preferred_element_type=jnp.float32)
        square_row = column_to_row(square, 0, LANES)
        for target in range(slices):
            for tile in range(tiles):
                first = target * out_cols + tile * LANES
                zpart_s[turn, target, tile * cands : (tile + 1) * cands, :] = projected[
                    :, first : first + LANES
                ]
            zpart_s[turn, target, tiles * cands : tiles * cands + 1, :] = square_row
        for step in range(slices - 1, 0, -1):
            spread(turn, step).start()

    def finish(turn):
        landed(zgot_s.at[turn], zrecv_sem.at[turn])
        total = zpart_s[turn, mh]
        for step in range(1, slices):
            total = total + zgot_s[turn, step - 1]
        column = row_to_column(total[tiles * cands :, :], 0, cands)
        factor = 1.0 / jnp.sqrt(column / (width * slices) + 1e-6)
        for tile in range(tiles):
            piece = total[tile * cands : (tile + 1) * cands] * factor
            out_ref[turn, :, tile * LANES : (tile + 1) * LANES] = piece.astype(out_ref.dtype)

    first = 0
    ready = {turn: 0 for turn in range(local)}
    done = 0
    for index, group in enumerate(groups):
        slots = list(range(first, first + len(group)))
        first += len(group)
        landed(kv_s.at[slots[0] : slots[-1] + 1], kv_sem.at[index])
        attend(slots)
        if index == 0:
            pl.semaphore_wait(barrier, seqs - 1 + slices - 1)
        for turn, step in group:
            ready[turn] += 1
            if step:
                exchange(turn, step).start()
        if first >= START * len(order) // 16 and ready[done] == seqs and index < len(groups) - 1:
            combine(done)
            done += 1
    while done < local:
        combine(done)
        done += 1
    for turn in range(local):
        finish(turn)
    landed(got_s, send_sem)
    landed(zgot_s, zsend_sem)


def body(
    query,
    new_key,
    new_value,
    keys,
    values,
    lengths,
    time_bucket,
    action,
    time_bias,
    action_bias,
    gate,
    norm_gain,
    w_out,
):
    users, block, width = keys.shape
    cands = query.shape[1]
    heads = time_bias.shape[1]
    size = width // heads
    seqs = lax.axis_size("seq")
    slices = lax.axis_size("head")
    local = users // seqs
    rows = heads * cands
    out_cols = w_out.shape[1] // slices
    tiles = out_cols // LANES
    groups = len(plan(seqs, local))
    dims = (users, cands, block, heads, size, seqs, slices, local, out_cols)
    f32, bf16 = jnp.float32, jnp.bfloat16
    anywhere = pl.BlockSpec(memory_space=pltpu.HBM)
    return pl.pallas_call(
        functools.partial(kernel, dims),
        out_shape=jax.ShapeDtypeStruct((local, cands, out_cols), bf16),
        in_specs=[anywhere] * 13,
        out_specs=pl.BlockSpec(memory_space=pltpu.VMEM),
        scratch_shapes=[
            pltpu.SMEM((users,), jnp.int32),
            pltpu.VMEM((users, cands, width), bf16),
            pltpu.VMEM((3, local, cands, width), bf16),
            pltpu.VMEM((users, 2, block, width), bf16),
            pltpu.VMEM((2, users, block), jnp.int32),
            pltpu.VMEM(time_bias.T.shape, f32),
            pltpu.VMEM(action_bias.T.shape, f32),
            pltpu.VMEM((width,), f32),
            pltpu.VMEM(w_out.shape, bf16),
            pltpu.VMEM((users, rows, width), bf16),
            pltpu.VMEM((local, cands, width), f32),
            pltpu.VMEM((heads, users, block), f32),
            pltpu.VMEM((local, seqs, rows + 1, size), f32),
            pltpu.VMEM((local, seqs - 1, rows + 1, size), f32),
            pltpu.VMEM((local, slices, tiles * cands + 1, LANES), f32),
            pltpu.VMEM((local, slices - 1, tiles * cands + 1, LANES), f32),
            pltpu.SemaphoreType.DMA((groups,)),
            pltpu.SemaphoreType.DMA((5,)),
            pltpu.SemaphoreType.DMA((3,)),
            pltpu.SemaphoreType.DMA,
            pltpu.SemaphoreType.DMA((local,)),
            pltpu.SemaphoreType.DMA,
            pltpu.SemaphoreType.DMA((local,)),
        ],
        compiler_params=pltpu.CompilerParams(
            collective_id=0, has_side_effects=True, vmem_limit_bytes=52428800
        ),
    )(
        *(
            pltpu.with_memory_space_constraint(x, pltpu.HBM)
            for x in (
                lengths,
                query,
                new_key,
                new_value,
                keys,
                values,
                time_bucket,
                action,
                time_bias.T,
                action_bias.T,
                gate,
                norm_gain,
                w_out,
            )
        )
    )


def solution(mesh):
    placed = (
        P("groups", None, "head"),
        P("groups", None, "head"),
        P("groups", None, "head"),
        P("groups", "seq", "head"),
        P("groups", "seq", "head"),
        P("groups"),
        P("groups", "seq"),
        P("groups", "seq"),
        P(None, "head"),
        P(None, "head"),
        P("groups", None, "head"),
        P("head"),
        P("head", None),
    )
    return jax.shard_map(
        body,
        mesh=mesh,
        in_specs=placed,
        out_specs=P(("groups", "seq"), None, "head"),
        check_vma=False,
    )
```

time: 21.5 us -> 19.7 us (0.916)
  Pallas kernels: 20.7 us -> 18.9 us
    pallas_call x1, Pallas kernels: 20.7 us -> 18.9 us  [body(): pl.pallas_call(functools.partial(kernel, dims), out_shape=jax.ShapeDtypeS...]
where the time goes in v2:
time: 19.7 us; the launch traced here: 19.5 us
  Pallas kernels  18.9 us (96%)
  local copies, waits for them, and re-layouts  0.62 us (3%)
    pallas_call x1, Pallas kernels, body(): pl.pallas_call(functools.partial(kernel, dims), out_shape=jax.ShapeDtypeS...  18.9 us
    unnamed x1, local copies, waits for them, and re-layouts  0.62 us

profile of v2, /device:TPU:0, one launch (start us, length us, event | category | flops | bytes accessed | tf_op | source)
XLA Modules:
  0.0 19.5 jit_solution(9308253805965325630)
XLA Ops:
  0.0 18.9 %shard_map.127 = bf16[4,16,256]{2,1,0:T(8,128)(2,1)S(1)} custom-call(s32[16]{0:T(128)} %len_hbm.1, bf16[16,16,256]{2,1,0:T(8,128)(2,1)} %q_hbm.1, bf16[16,16,256]{2,1,0:T(8,128)(2,1)} %nk_hbm.1, bf16[16,16,256]{2,1,0:T(8,128)(2,1)} %nv_hbm.1, bf16[16,1024,256]{2,1,0:T(8,128)(2,1)} %k_hbm.1, bf16[16,1024,256]{2,1,0:T(8,128)(2,1)} %v_hbm.1, ...), custom_call_target="tpu_custom_call" | custom-call | tf_op jit(solution)/shard_map/pallas_call | solution.py:361
  18.9 0.6 %copy.15 = bf16[4,16,256]{2,1,0:T(8,128)(2,1)} copy(bf16[4,16,256]{2,1,0:T(8,128)(2,1)S(1)} %shard_map.127) | data formatting | bytes 65536

commit v3 on v2

--- a/solution.py
+++ b/solution.py
@@ -11,8 +11,8 @@
 MESH = pl.DeviceIdType.MESH
 LANES = 128
 LOG2E = math.log2(math.e)
-GROUP = 4
-START = 13
+GROUP = 3
+START = 11
 INVALID = -1e30
 FLOOR = -1e29
 NT = (((1,), (1,)), ((), ()))
@@ -28,14 +28,30 @@
 
 
 def plan(seqs, local):
-    away = list(range(seqs - 1, 0, -1))
-    groups = []
-    for turn in range(local):
-        steps = away + [0] if turn == 0 else away
-        for first in range(0, len(steps), GROUP):
-            groups.append([(turn, step) for step in steps[first : first + GROUP]])
-    groups.extend([(turn, 0)] for turn in range(1, local))
-    return groups
+    far = range(seqs - 1, 1, -1)
+    near = [step for step in (1, 0) if step < seqs]
+    order = [(0, step) for step in far]
+    for turn in range(1, local):
+        if near and turn <= len(near):
+            order.append((0, near[turn - 1]))
+        order += [(turn, step) for step in far]
+    order += [(0, step) for step in near[max(local - 1, 0) :]]
+    order += [(turn, step) for step in near for turn in range(1, local)]
+    groups, first = [], 0
+    while first < len(order):
+        size = GROUP if first else GROUP - 1
+        groups.append(order[first : first + size])
+        first += size
+    acts, taken, ready, done = [], 0, [0] * local, 0
+    for group in groups:
+        acts.append(group)
+        taken += len(group)
+        for turn, _ in group:
+            ready[turn] += 1
+        if taken < len(order) and 16 * taken >= START * len(order) and ready[done] == seqs:
+            acts.append(done)
+            done += 1
+    return acts + list(range(done, local))
 
 
 def column_to_row(column, first, lanes):
@@ -143,7 +159,9 @@
     for copy in early:
         copy.start()
     order = []
-    groups = plan(seqs, local)
+    acts = plan(seqs, local)
+    groups = [act for act in acts if isinstance(act, list)]
+    starts = [sum(len(group) for group in groups[:index]) for index in range(len(groups))]
     for index, group in enumerate(groups):
         for turn, step in group:
             user = partner(me, step, seqs) * local + turn
@@ -229,15 +247,6 @@
             held = slice(head * cands, (head + 1) * cands)
             piece = mixed[held, head * size : (head + 1) * size]
             part_s[turn, step, held, :] = piece if fresh is None else piece + fresh[held]
-
-    def attend(slots):
-        waiting = []
-        for slot in slots:
-            waiting.append((slot, *score(slot)))
-            if len(waiting) > 1:
-                mix(*waiting.pop(0))
-        for item in waiting:
-            mix(*item)
 
     def exchange(turn, step):
         return pltpu.make_async_remote_copy(
@@ -303,26 +312,25 @@
             piece = total[tile * cands : (tile + 1) * cands] * factor
             out_ref[turn, :, tile * LANES : (tile + 1) * LANES] = piece.astype(out_ref.dtype)
 
-    first = 0
-    ready = {turn: 0 for turn in range(local)}
-    done = 0
-    for index, group in enumerate(groups):
-        slots = list(range(first, first + len(group)))
-        first += len(group)
-        landed(kv_s.at[slots[0] : slots[-1] + 1], kv_sem.at[index])
-        attend(slots)
+    index = 0
+    for act in acts:
+        if isinstance(act, int):
+            combine(act)
+            continue
+        first, last = starts[index], starts[index] + len(act)
+        landed(kv_s.at[first:last], kv_sem.at[index])
+        waiting = []
+        for slot in range(first, last):
+            waiting.append((slot, *score(slot)))
+            if len(waiting) > 1:
+                mix(*waiting.pop(0))
+        mix(*waiting.pop(0))
         if index == 0:
             pl.semaphore_wait(barrier, seqs - 1 + slices - 1)
-        for turn, step in group:
-            ready[turn] += 1
+        for turn, step in act:
             if step:
                 exchange(turn, step).start()
-        if first >= START * len(order) // 16 and ready[done] == seqs and index < len(groups) - 1:
-            combine(done)
-            done += 1
-    while done < local:
-        combine(done)
-        done += 1
+        index += 1
     for turn in range(local):
         finish(turn)
     landed(got_s, send_sem)
@@ -354,7 +362,7 @@
     rows = heads * cands
     out_cols = w_out.shape[1] // slices
     tiles = out_cols // LANES
-    groups = len(plan(seqs, local))
+    groups = len([act for act in plan(seqs, local) if isinstance(act, list)])
     dims = (users, cands, block, heads, size, seqs, slices, local, out_cols)
     f32, bf16 = jnp.float32, jnp.bfloat16
     anywhere = pl.BlockSpec(memory_space=pltpu.HBM)

time: 19.7 us -> 18.3 us (0.929)
  Pallas kernels: 18.9 us -> 17.6 us
    pallas_call x1, Pallas kernels: 18.9 us -> 17.6 us  [body(): pl.pallas_call(functools.partial(kernel, dims), out_shape=jax.ShapeDtypeS...]
where the time goes in v3:
time: 18.3 us; the launch traced here: 18.2 us
  Pallas kernels  17.6 us (96%)
  local copies, waits for them, and re-layouts  0.62 us (3%)
    pallas_call x1, Pallas kernels, body(): pl.pallas_call(functools.partial(kernel, dims), out_shape=jax.ShapeDtypeS...  17.6 us
    unnamed x1, local copies, waits for them, and re-layouts  0.62 us

profile of v3, /device:TPU:0, one launch (start us, length us, event | category | flops | bytes accessed | tf_op | source)
XLA Modules:
  0.0 18.2 jit_solution(3321174998231052737)
XLA Ops:
  0.0 17.6 %shard_map.127 = bf16[4,16,256]{2,1,0:T(8,128)(2,1)S(1)} custom-call(s32[16]{0:T(128)} %len_hbm.1, bf16[16,16,256]{2,1,0:T(8,128)(2,1)} %q_hbm.1, bf16[16,16,256]{2,1,0:T(8,128)(2,1)} %nk_hbm.1, bf16[16,16,256]{2,1,0:T(8,128)(2,1)} %nv_hbm.1, bf16[16,1024,256]{2,1,0:T(8,128)(2,1)} %k_hbm.1, bf16[16,1024,256]{2,1,0:T(8,128)(2,1)} %v_hbm.1, ...), custom_call_target="tpu_custom_call" | custom-call | tf_op jit(solution)/shard_map/pallas_call | solution.py:369
  17.6 0.6 %copy.15 = bf16[4,16,256]{2,1,0:T(8,128)(2,1)} copy(bf16[4,16,256]{2,1,0:T(8,128)(2,1)S(1)} %shard_map.127) | data formatting | bytes 65536

commit v4 on v3

--- a/solution.py
+++ b/solution.py
@@ -12,7 +12,9 @@
 LANES = 128
 LOG2E = math.log2(math.e)
 GROUP = 3
+SIZES = [2, 3, 4, 2]
 START = 11
+DEFER = 2
 INVALID = -1e30
 FLOOR = -1e29
 NT = (((1,), (1,)), ((), ()))
@@ -28,20 +30,18 @@
 
 
 def plan(seqs, local):
-    far = range(seqs - 1, 1, -1)
+    far = range(2, seqs)
     near = [step for step in (1, 0) if step < seqs]
-    order = [(0, step) for step in far]
-    for turn in range(1, local):
-        if near and turn <= len(near):
-            order.append((0, near[turn - 1]))
-        order += [(turn, step) for step in far]
-    order += [(0, step) for step in near[max(local - 1, 0) :]]
+    order = [(turn, step) for turn in range(min(local, 2)) for step in far]
+    order += [(0, step) for step in near[:-1]]
+    order += [(turn, step) for turn in range(2, local) for step in far]
+    order += [(0, step) for step in near[-1:]]
     order += [(turn, step) for step in near for turn in range(1, local)]
     groups, first = [], 0
-    while first < len(order):
-        size = GROUP if first else GROUP - 1
-        groups.append(order[first : first + size])
-        first += size
+    for size in SIZES + [GROUP] * len(order):
+        if first < len(order):
+            groups.append(order[first : first + size])
+            first += size
     acts, taken, ready, done = [], 0, [0] * local, 0
     for group in groups:
         acts.append(group)
@@ -258,16 +258,25 @@
             device_id_type=MESH,
         )
 
-    def spread(turn, step):
-        target = partner(mh, step, slices)
+    def receiver(rank):
+        first = (slices - mh) // slices
+        if rank == 0:
+            return first * (slices - 1)
+        below = slices - rank - 1
+        return below + (below - mh - first * slices + 2 * slices) // (2 * slices)
+
+    def spread(turn, rank):
+        target = receiver(rank)
         return pltpu.make_async_remote_copy(
             src_ref=zpart_s.at[turn, target],
-            dst_ref=zgot_s.at[turn, step - 1],
+            dst_ref=zgot_s.at[turn, mh - (mh - target - 1 + slices) // slices],
             send_sem=zsend_sem,
             recv_sem=zrecv_sem.at[turn],
             device_id={"head": target},
             device_id_type=MESH,
         )
+
+    later = []
 
     def combine(turn):
         landed(got_s.at[turn], recv_sem.at[turn])
@@ -298,8 +307,13 @@
                     :, first : first + LANES
                 ]
             zpart_s[turn, target, tiles * cands : tiles * cands + 1, :] = square_row
-        for step in range(slices - 1, 0, -1):
-            spread(turn, step).start()
+        spread(turn, 0).start()
+        later.append(turn)
+        if turn == local - 1 or turn < local - DEFER:
+            for held in later:
+                for rank in range(1, slices - 1):
+                    spread(held, rank).start()
+            later.clear()
 
     def finish(turn):
         landed(zgot_s.at[turn], zrecv_sem.at[turn])

time: 18.3 us -> 17.1 us (0.934)
  Pallas kernels: 17.6 us -> 16.3 us
    pallas_call x1, Pallas kernels: 17.6 us -> 16.3 us  [body(): pl.pallas_call(functools.partial(kernel, dims), out_shape=jax.ShapeDtypeS...]
where the time goes in v4:
time: 17.1 us; the launch traced here: 17 us
  Pallas kernels  16.3 us (95%)
  local copies, waits for them, and re-layouts  0.62 us (4%)
    pallas_call x1, Pallas kernels, body(): pl.pallas_call(functools.partial(kernel, dims), out_shape=jax.ShapeDtypeS...  16.3 us
    unnamed x1, local copies, waits for them, and re-layouts  0.62 us

profile of v4, /device:TPU:0, one launch (start us, length us, event | category | flops | bytes accessed | tf_op | source)
XLA Modules:
  0.0 17.0 jit_solution(14795970413656834342)
XLA Ops:
  0.0 16.3 %shard_map.127 = bf16[4,16,256]{2,1,0:T(8,128)(2,1)S(1)} custom-call(s32[16]{0:T(128)} %len_hbm.1, bf16[16,16,256]{2,1,0:T(8,128)(2,1)} %q_hbm.1, bf16[16,16,256]{2,1,0:T(8,128)(2,1)} %nk_hbm.1, bf16[16,16,256]{2,1,0:T(8,128)(2,1)} %nv_hbm.1, bf16[16,1024,256]{2,1,0:T(8,128)(2,1)} %k_hbm.1, bf16[16,1024,256]{2,1,0:T(8,128)(2,1)} %v_hbm.1, ...), custom_call_target="tpu_custom_call" | custom-call | tf_op jit(solution)/shard_map/pallas_call | solution.py:383
  16.3 0.6 %copy.15 = bf16[4,16,256]{2,1,0:T(8,128)(2,1)} copy(bf16[4,16,256]{2,1,0:T(8,128)(2,1)S(1)} %shard_map.127) | data formatting | bytes 65536

commit v5 on v4

--- a/solution.py
+++ b/solution.py
@@ -15,6 +15,7 @@
 SIZES = [2, 3, 4, 2]
 START = 11
 DEFER = 2
+WHEN = 4
 INVALID = -1e30
 FLOOR = -1e29
 NT = (((1,), (1,)), ((), ()))
@@ -145,11 +146,10 @@
     ]
     mine = pl.ds(me * local, local)
     late = [
-        pltpu.make_async_copy(source, target, late_sem.at[min(i, 2)])
+        pltpu.make_async_copy(source, target, late_sem.at[min(i, 1)])
         for i, (source, target) in enumerate(
             (
                 (gain_hbm, gain_s),
-                (w_hbm, w_s),
                 (nk_hbm.at[mine], mine_s.at[0]),
                 (nv_hbm.at[mine], mine_s.at[1]),
                 (gate_hbm.at[mine], mine_s.at[2]),
@@ -162,7 +162,10 @@
     acts = plan(seqs, local)
     groups = [act for act in acts if isinstance(act, list)]
     starts = [sum(len(group) for group in groups[:index]) for index in range(len(groups))]
+    w_copy = pltpu.make_async_copy(w_hbm, w_s, late_sem.at[2])
     for index, group in enumerate(groups):
+        if index == min(WHEN, len(groups) - 1):
+            w_copy.start(priority=1)
         for turn, step in group:
             user = partner(me, step, seqs) * local + turn
             for part, source in enumerate((k_hbm, v_hbm)):
@@ -202,9 +205,8 @@
             )
             bias_s[head, :, lanes] = jnp.where(limit > chunk * LANES, bias, INVALID)
 
-    for copy in late[:2]:
-        copy.wait()
-    landed(mine_s, late_sem.at[2])
+    late[0].wait()
+    landed(mine_s, late_sem.at[1])
     gate = mine_s[2].astype(jnp.float32)
     gated_s[...] = gain_s[...].reshape(1, 1, width) * (gate / (1.0 + jnp.exp(-gate)))
 
@@ -329,6 +331,8 @@
     index = 0
     for act in acts:
         if isinstance(act, int):
+            if act == 0:
+                w_copy.wait()
             combine(act)
             continue
         first, last = starts[index], starts[index] + len(act)

time: 17.1 us -> 17 us (level)
  no operation moved by 1% of the time
where the time goes in v5:
time: 17 us; the launch traced here: 16.9 us
  Pallas kernels  16.2 us (95%)
  local copies, waits for them, and re-layouts  0.62 us (4%)
    pallas_call x1, Pallas kernels, body(): pl.pallas_call(functools.partial(kernel, dims), out_shape=jax.ShapeDtypeS...  16.2 us
    unnamed x1, local copies, waits for them, and re-layouts  0.62 us

profile of v5, /device:TPU:0, one launch (start us, length us, event | category | flops | bytes accessed | tf_op | source)
XLA Modules:
  0.0 16.9 jit_solution(6098358477446853370)
XLA Ops:
  0.0 16.2 %shard_map.127 = bf16[4,16,256]{2,1,0:T(8,128)(2,1)S(1)} custom-call(s32[16]{0:T(128)} %len_hbm.1, bf16[16,16,256]{2,1,0:T(8,128)(2,1)} %q_hbm.1, bf16[16,16,256]{2,1,0:T(8,128)(2,1)} %nk_hbm.1, bf16[16,16,256]{2,1,0:T(8,128)(2,1)} %nv_hbm.1, bf16[16,1024,256]{2,1,0:T(8,128)(2,1)} %k_hbm.1, bf16[16,1024,256]{2,1,0:T(8,128)(2,1)} %v_hbm.1, ...), custom_call_target="tpu_custom_call" | custom-call | tf_op jit(solution)/shard_map/pallas_call | solution.py:387
  16.2 0.6 %copy.15 = bf16[4,16,256]{2,1,0:T(8,128)(2,1)} copy(bf16[4,16,256]{2,1,0:T(8,128)(2,1)S(1)} %shard_map.127) | data formatting | bytes 65536

commit v6 on v5

--- a/solution.py
+++ b/solution.py
@@ -205,11 +205,6 @@
             )
             bias_s[head, :, lanes] = jnp.where(limit > chunk * LANES, bias, INVALID)
 
-    late[0].wait()
-    landed(mine_s, late_sem.at[1])
-    gate = mine_s[2].astype(jnp.float32)
-    gated_s[...] = gain_s[...].reshape(1, 1, width) * (gate / (1.0 + jnp.exp(-gate)))
-
     def by_head(source):
         return jnp.concatenate(
             [source[:, head * size : (head + 1) * size] for head in range(heads)], axis=0
@@ -312,8 +307,8 @@
         spread(turn, 0).start()
         later.append(turn)
         if turn == local - 1 or turn < local - DEFER:
-            for held in later:
-                for rank in range(1, slices - 1):
+            for rank in range(1, slices - 1):
+                for held in later:
                     spread(held, rank).start()
             later.clear()
 
@@ -348,6 +343,11 @@
         for turn, step in act:
             if step:
                 exchange(turn, step).start()
+        if index == 0:
+            late[0].wait()
+            landed(mine_s, late_sem.at[1])
+            gate = mine_s[2].astype(jnp.float32)
+            gated_s[...] = gain_s[...].reshape(1, 1, width) * (gate / (1.0 + jnp.exp(-gate)))
         index += 1
     for turn in range(local):
         finish(turn)

time: 17 us -> 17 us (level)
  no operation moved by 1% of the time
where the time goes in v6:
time: 17 us; the launch traced here: 16.9 us
  Pallas kernels  16.2 us (95%)
  local copies, waits for them, and re-layouts  0.62 us (4%)
    pallas_call x1, Pallas kernels, body(): pl.pallas_call(functools.partial(kernel, dims), out_shape=jax.ShapeDtypeS...  16.2 us
    unnamed x1, local copies, waits for them, and re-layouts  0.62 us

profile of v6, /device:TPU:0, one launch (start us, length us, event | category | flops | bytes accessed | tf_op | source)
XLA Modules:
  0.0 16.9 jit_solution(10692308754616948279)
XLA Ops:
  0.0 16.2 %shard_map.127 = bf16[4,16,256]{2,1,0:T(8,128)(2,1)S(1)} custom-call(s32[16]{0:T(128)} %len_hbm.1, bf16[16,16,256]{2,1,0:T(8,128)(2,1)} %q_hbm.1, bf16[16,16,256]{2,1,0:T(8,128)(2,1)} %nk_hbm.1, bf16[16,16,256]{2,1,0:T(8,128)(2,1)} %nv_hbm.1, bf16[16,1024,256]{2,1,0:T(8,128)(2,1)} %k_hbm.1, bf16[16,1024,256]{2,1,0:T(8,128)(2,1)} %v_hbm.1, ...), custom_call_target="tpu_custom_call" | custom-call | tf_op jit(solution)/shard_map/pallas_call | solution.py:387
  16.2 0.6 %copy.15 = bf16[4,16,256]{2,1,0:T(8,128)(2,1)} copy(bf16[4,16,256]{2,1,0:T(8,128)(2,1)S(1)} %shard_map.127) | data formatting | bytes 65536
